TPU v7x, 32 devices: a whole 2x2x4 slice. The times are simulated.
32 devices in a mesh: ctx: 16 (over z, x, core), wt: 2 (over y).
Axes of the slice: x: 2, y: 2, z: 4, core: 2. Of those that a mesh axis runs over, the one named last changes fastest.
Arguments:
- patches: bfloat16 [8192, 1280], P('ctx'), may hold values from -6 to 6
- vit_gain: float32 [1280], replicated, may hold values from 0.5 to 1.5
- vit_codes: bfloat16 [1280, 3, 1280], P(None, None, 'wt'), may hold values from -1 to 1
- vit_scales: bfloat16 [2], P('wt'), may hold values from 0.5 to 2
- vit_bias: float32 [3, 1280], P(None, 'wt'), may hold values from -3 to 3
- window_ids: int32 [8192], P('ctx'), may hold values from 63 to 8191, as said below
- merger_codes: bfloat16 [4, 1280, 8192], P(None, 'wt', 'ctx'), may hold values from -0.078125 to 0.078125
- merger_scales: bfloat16 [1, 2, 8192], P(None, 'wt', 'ctx'), may hold values from 0.5 to 2
- merger_bias: float32 [8192], P('wt'), may hold values from -3 to 3
- positions: int32 [2048], P('ctx'), may hold values from 0 to 8191, as said below
- text_embed: bfloat16 [8192, 8192], P('ctx', 'wt'), may hold values from -6 to 6
- norm_gain: float32 [8192], P('wt'), may hold values from 0.5 to 1.5
- llm_codes: bfloat16 [8192, 8, 768], P('wt', None, 'ctx'), may hold values from -1 to 1
- llm_scales: bfloat16 [2, 8, 768], P('wt', None, 'ctx'), may hold values from 0.5 to 2
- llm_bias: float32 [8, 768], P('wt'), may hold values from -3 to 3
- segments: int32 [8192], P('ctx'), may hold values from 0 to 7, never falling along the last dimension, each value on 1 to 2048 neighbouring positions
Outputs:
- attention_out: bfloat16 [8192, 4096], P('ctx', 'wt')
Inputs may be any that keep to these rules, and one draw needn't show every extreme that they name: `window_ids`: windows are runs of consecutive patches of at most 64, never crossing a block of 512 patches; patches of one window share the id, different windows have different ids. `positions`: distinct. The 128 entries of one aligned block (one device's merged tokens) put at most 16 into any one block of 512 positions, and exactly 16 into some block. `segments`: never falling; each run of equal ids is at most 2048 positions long.
All inputs are finite; a program needn't handle non-finite values.
Results may differ from a plain program's by a relative error of at most 0.025.
Values may be sent and summed in bfloat16 or wider, within the bound.
No kernel may reach another device: no remote copies, remote signals or barrier semaphores. Data moves between devices by JAX's collectives and lax.ppermute only.
A program may use at most 192 MiB of HBM per device.

v0:
```python
import jax
import jax.numpy as jnp
from jax import lax
from jax.sharding import PartitionSpec as P

VHD = 80
D = 8192
KVH = 8
HD = 128
GROUP = 4
MERGE = 4
REACH = 4
VIT_EPS = 1e-06
RMS_EPS = 1e-06
ROPE_BASE = 1000000.0
FILL_LOW = -1e30


def passed_along(value, axis, steps):
    count = lax.axis_size(axis)
    leading, last = (max(0, -steps), min(count, count - steps))
    return lax.ppermute(value, axis, [(source, source + steps) for source in range(leading, last)])


def softmax_rows(scores, allowed):
    masked = jnp.where(allowed, scores, FILL_LOW)
    highest = jnp.max(masked, axis=-1, keepdims=True)
    raised = jnp.exp(masked - highest)
    return raised / jnp.sum(raised, axis=-1, keepdims=True)


def vision_norm_rows(patches, vit_gain):
    values = patches.astype(jnp.float32)
    mean_square = jnp.mean(values * values, axis=1, keepdims=True)
    return (values * lax.rsqrt(mean_square + VIT_EPS) * vit_gain).astype(jnp.bfloat16)


def window_attention(normed, weight_block, bias_block, window_ids):
    row_count = normed.shape[0]
    packed = jnp.dot(
        normed, weight_block.reshape(normed.shape[1], -1), preferred_element_type=jnp.float32
    )
    triple = (packed.reshape(row_count, 3, -1) + bias_block).astype(jnp.bfloat16)
    heads_here = triple.shape[2] // VHD
    queries = triple[:, 0].reshape(row_count, heads_here, VHD)
    keys_here = triple[:, 1].reshape(row_count, heads_here, VHD)
    values_here = triple[:, 2].reshape(row_count, heads_here, VHD)
    scores = jnp.einsum(
        "qhd,khd->hqk", queries, keys_here, preferred_element_type=jnp.float32
    ) * VHD ** (-0.5)
    allowed = window_ids[:, None] == window_ids[None, :]
    softmaxed = softmax_rows(scores, allowed[None]).astype(jnp.bfloat16)
    blended = jnp.einsum("hqk,khd->qhd", softmaxed, values_here, preferred_element_type=jnp.float32)
    return blended.astype(jnp.bfloat16).reshape(row_count, -1)


def rope_tables(first, length):
    places = (first + jnp.arange(length, dtype=jnp.int32)).astype(jnp.float32)
    frequency = ROPE_BASE ** (-jnp.arange(0, HD, 2).astype(jnp.float32) / HD)
    angles = places[:, None] * frequency[None, :]
    angles = jnp.concatenate([angles, angles], axis=1)
    return (jnp.cos(angles), jnp.sin(angles))


def rotary(inputs, cosine, sine):
    halfway = inputs.shape[-1] // 2
    turned = jnp.concatenate([-inputs[..., halfway:], inputs[..., :halfway]], axis=-1)
    return inputs * cosine + turned * sine


def split_heads(triple, cosine, sine):
    row_count, group_count = (triple.shape[0], triple.shape[1])
    queries = triple[:, :, : GROUP * HD].reshape(row_count, group_count, GROUP, HD)
    queries = rotary(queries, cosine[:, None, None, :], sine[:, None, None, :]).astype(jnp.bfloat16)
    keys_rot = rotary(
        triple[:, :, GROUP * HD : (GROUP + 1) * HD], cosine[:, None, :], sine[:, None, :]
    ).astype(jnp.bfloat16)
    values_cut = triple[:, :, (GROUP + 1) * HD :].astype(jnp.bfloat16)
    return (queries, keys_rot, values_cut)


def merge_project(features, merger_codes, merger_scales, merger_bias):
    row_count = features.shape[0]
    flat = features.reshape(row_count, -1)
    codes_piece = lax.all_gather(merger_codes, "ctx", axis=2, tiled=True)
    scale_piece = lax.all_gather(merger_scales, "ctx", axis=2, tiled=True)
    width = codes_piece.shape[2]
    dequant = (codes_piece.astype(jnp.float32) * scale_piece.astype(jnp.float32)).astype(
        jnp.bfloat16
    )
    product = jnp.dot(flat, dequant.reshape(-1, width), preferred_element_type=jnp.float32)
    mine = lax.psum_scatter(
        product.astype(jnp.bfloat16), "wt", scatter_dimension=1, tiled=True
    ).astype(jnp.float32)
    return (mine + merger_bias).astype(jnp.bfloat16)


def route_tokens(values, positions, span):
    owners = lax.axis_size("ctx")
    items = values.shape[0]
    capacity = 2 * positions.shape[0] // owners
    target = positions // span
    item_order = jnp.arange(items, dtype=jnp.int32)
    before = (target[None, :] == target[:, None]) & (item_order[None, :] < item_order[:, None])
    ranks = jnp.sum(before.astype(jnp.int32), axis=1)
    slots = target * capacity + ranks
    table = slots[None, :] == jnp.arange(owners * capacity, dtype=jnp.int32)[:, None]
    packed = jnp.dot(table.astype(jnp.bfloat16), values, preferred_element_type=jnp.float32).astype(
        jnp.bfloat16
    )
    labels = jnp.sum(jnp.where(table, positions[None, :] + 1, 0), axis=1) - 1
    return (
        lax.all_to_all(packed, "ctx", split_axis=0, concat_axis=0, tiled=True),
        lax.all_to_all(labels, "ctx", split_axis=0, concat_axis=0, tiled=True),
    )


def place_tokens(text_embed, arrived, labels, first):
    local = labels - first
    table = local[None, :] == jnp.arange(text_embed.shape[0], dtype=jnp.int32)[:, None]
    filled = jnp.dot(
        table.astype(jnp.bfloat16), arrived, preferred_element_type=jnp.float32
    ).astype(jnp.bfloat16)
    covered = jnp.any(table, axis=1)
    return jnp.where(covered[:, None], filled, text_embed)


def on_device(
    patches,
    vit_gain,
    vit_codes,
    vit_scales,
    vit_bias,
    window_ids,
    merger_codes,
    merger_scales,
    merger_bias,
    positions,
    text_embed,
    norm_gain,
    llm_codes,
    llm_scales,
    llm_bias,
    segments,
):
    row_count = text_embed.shape[0]
    first = lax.axis_index("ctx") * row_count
    normed_patches = vision_norm_rows(patches, vit_gain)
    vit_weight = (vit_codes.astype(jnp.float32) * vit_scales.astype(jnp.float32)[0]).astype(
        jnp.bfloat16
    )
    attended = window_attention(normed_patches, vit_weight, vit_bias, window_ids)
    token_count = positions.shape[0]
    features = attended.reshape(token_count, MERGE, -1)
    projected = merge_project(features, merger_codes, merger_scales, merger_bias)
    embedded, labels = route_tokens(projected, positions, row_count)
    hidden = place_tokens(text_embed, embedded, labels, first)
    values = hidden.astype(jnp.float32)
    squares = lax.psum(jnp.sum(values * values, axis=1), "wt")
    normed = (values * lax.rsqrt(squares[:, None] / D + RMS_EPS) * norm_gain).astype(jnp.bfloat16)
    local_rows = normed.shape[1]
    codes_piece = lax.all_gather(llm_codes, "ctx", axis=2, tiled=True)
    scale_piece = lax.all_gather(llm_scales, "ctx", axis=2, tiled=True)
    width = codes_piece.shape[2]
    dequant_piece = (codes_piece.astype(jnp.float32) * scale_piece.astype(jnp.float32)).astype(
        jnp.bfloat16
    )
    product = jnp.dot(
        normed, dequant_piece.reshape(local_rows, -1), preferred_element_type=jnp.float32
    )
    partial_value = product.reshape(row_count, KVH, width)
    triple = (
        lax.psum_scatter(
            partial_value.astype(jnp.bfloat16), "wt", scatter_dimension=1, tiled=True
        ).astype(jnp.float32)
        + llm_bias
    )
    cosine, sine = rope_tables(first, row_count)
    queries, keys_rot, values_cut = split_heads(triple, cosine, sine)
    own = (keys_rot, values_cut, segments)
    arrivals = [own]
    moving = own
    for distance in range(REACH):
        moving = passed_along((moving[0], moving[1], moving[2]), "ctx", 1)
        arrivals.append(moving)
    keys_all = jnp.concatenate([arrival[0] for arrival in arrivals], axis=0)
    values_all = jnp.concatenate([arrival[1] for arrival in arrivals], axis=0)
    key_segments = jnp.concatenate([arrival[2] for arrival in arrivals], axis=0)
    key_places = jnp.concatenate(
        [
            first - distance * row_count + jnp.arange(row_count, dtype=jnp.int32)
            for distance in range(REACH + 1)
        ],
        axis=0,
    )
    query_places = first + jnp.arange(row_count, dtype=jnp.int32)
    allowed = (
        (segments[:, None] == key_segments[None, :])
        & (key_places[None, :] <= query_places[:, None])
        & (key_places[None, :] >= 0)
    )
    outputs = []
    for group_index in range(queries.shape[1]):
        scores = jnp.einsum(
            "qjd,kd->jqk",
            queries[:, group_index],
            keys_all[:, group_index],
            preferred_element_type=jnp.float32,
        ) * HD ** (-0.5)
        softmaxed = softmax_rows(scores, allowed[None]).astype(jnp.bfloat16)
        blended = jnp.einsum(
            "jqk,kd->qjd", softmaxed, values_all[:, group_index], preferred_element_type=jnp.float32
        )
        outputs.append(blended.astype(jnp.bfloat16).reshape(row_count, -1))
    return jnp.concatenate(outputs, axis=1)


def solution(mesh):
    in_specs = (
        P("ctx", None),
        P(),
        P(None, None, "wt"),
        P("wt"),
        P(None, "wt"),
        P("ctx"),
        P(None, "wt", "ctx"),
        P(None, "wt", "ctx"),
        P("wt"),
        P("ctx"),
        P("ctx", "wt"),
        P("wt"),
        P("wt", None, "ctx"),
        P("wt", None, "ctx"),
        P("wt", None),
        P("ctx"),
    )
    out_specs = P("ctx", "wt")
    return jax.shard_map(
        on_device, mesh=mesh, in_specs=in_specs, out_specs=out_specs, check_vma=False
    )
```

profile of v0, /device:TPU:1, one launch (start us, length us, event | category | flops | bytes accessed | tf_op | source)
XLA Modules:
  0.0 852.8 jit_solution(12550410183688036739)
XLA Ops:
  7.3 8.3 copy.82
  16.6 6.4 add_convert_fusion
  24.2 5.5 fusion.104
  36.8 23.8 %all_gather.13 = bf16[1,1,8192]{2,1,0:T(2,128)(2,1)S(1)} all-gather(bf16[1,1,512]{2,1,0:T(2,128)(2,1)S(1)} %copy-done.10), channel_id=1, replica_groups=mesh['ctx'=16,'wt'=2] {'ctx'}, dimensions={2}, use_global_device_ids=true | all-gather | bytes 17408 | tf_op jit(solution)/shard_map/all_gather | solution.py:86
  60.6 158.5 %all-gather.3.cloned.1.call-done = bf16[4,640,8192]{2,1,0:T(8,128)(2,1)} async-done(((bf16[4,640,512]{2,1,0:T(8,128)(2,1)}), bf16[4,640,8192]{2,1,0:T(8,128)(2,1)}) %all-gather.3.cloned.1.call-update) | async-done | bytes 41943056 | tf_op jit(solution)/shard_map/all_gather | solution.py:85
  219.1 28.4 %multiply_convert_fusion.1 = bf16[4,640,8192]{2,1,0:T(8,128)(2,1)} fusion(bf16[4,640,8192]{2,1,0:T(8,128)(2,1)} %all-gather.3.cloned.1.call-done, f32[8192]{0:T(1024)S(1)} %bitcast.234), kind=kLoop, calls=%fused_computation.6 | loop fusion | flops 62914560 | bytes 83918848 | tf_op jit(solution)/shard_map/convert_element_type | solution.py:88
  247.4 17.2 %convolution_convert_fusion = bf16[128,8192]{1,0:T(8,128)(2,1)} fusion(bf16[128,2560]{1,0:T(8,128)(2,1)S(1)} %reshape_reshape_reshape.3, bf16[2560,8192]{1,0:T(8,128)(2,1)} %bitcast.224), kind=kOutput, calls=%fused_computation.45 | convolution fusion | flops 5369757696 | bytes 44695552 | tf_op jit(solution)/shard_map/dot_general | solution.py:91
  266.4 5.0 all-to-all-start
  271.4 24.8 %reduce-scatter.3.cloned.1.call-done = bf16[128,4096]{1,0:T(8,128)(2,1)} async-done(((bf16[128,8192]{1,0:T(8,128)(2,1)}), bf16[128,4096]{1,0:T(8,128)(2,1)}) %reduce-scatter.3.cloned.1.call-update) | async-done | bytes 1048592 | tf_op jit(solution)/shard_map/reduce_scatter | solution.py:92
  299.5 6.4 all-to-all-start.1
  306.1 87.5 %all_gather.15 = bf16[1,8,768]{1,0,2:T(2,128)(2,1)S(1)} all-gather(bf16[1,8,48]{1,0,2:T(2,128)(2,1)S(1)} %copy.88), channel_id=1, replica_groups=mesh['ctx'=16,'wt'=2] {'ctx'}, dimensions={2}, use_global_device_ids=true | all-gather | bytes 13056 | tf_op jit(solution)/shard_map/all_gather | solution.py:163
  394.4 4.9 fusion.29
  403.5 177.3 %all-gather.5.cloned.1.call-done = bf16[4096,8,768]{0,2,1:T(8,128)(2,1)} async-done(((bf16[4096,8,48]{0,2,1:T(8,128)(2,1)}), bf16[4096,8,768]{0,2,1:T(8,128)(2,1)}) %all-gather.5.cloned.1.call-update) | async-done | bytes 50331664 | tf_op jit(solution)/shard_map/all_gather | solution.py:162
  580.8 33.5 %fusion.48 = bf16[512,8,768]{2,0,1:T(8,128)(2,1)} fusion(bf16[4096,8,768]{0,2,1:T(8,128)(2,1)} %all-gather.5.cloned.1.call-done, f32[8,768]{1,0:T(8,128)S(1)} %copy.89, bf16[512,4096]{1,0:T(8,128)(2,1)} %get-tuple-element.25, f32[4096]{0:T(1024)S(1)} %copy-done.12, f32[512]{0:T(512)S(1)} %add_rsqrt_fusion), kind=kOutput, calls=%fused_computation.75 | convolution fusion | flops 25856835584 | bytes 60860416 | tf_op jit(solution)/shard_map/dot_general | solution.py:168
  623.8 13.5 %collective-permute-start.6 = (s32[512]{0:T(512)S(1)}, s32[512]{0:T(512)S(1)}, u32[]{:S(2)}, u32[]{:S(2)}) collective-permute-start(s32[512]{0:T(512)S(1)} %collective-permute-done.5), channel_id=1, source_target_pairs={{0,2},{2,4},{4,6},{6,8},{8,10},{10,12},{12,14},{14,16},{16,18},{18... | collective-permute-start | bytes 6152 | tf_op jit(solution)/shard_map/ppermute | solution.py:22
  642.9 58.9 %reduce-scatter.5.cloned.1.call-done = bf16[512,4,768]{2,0,1:T(8,128)(2,1)} async-done(((bf16[512,8,768]{2,0,1:T(8,128)(2,1)}), bf16[512,4,768]{2,0,1:T(8,128)(2,1)}) %reduce-scatter.5.cloned.1.call-update) | async-done | bytes 3145744 | tf_op jit(solution)/shard_map/reduce_scatter | solution.py:173
  756.3 12.6 %fusion.108 = (f32[4,512]{1,0:T(4,128)S(1)}, f32[4,512,2560]{1,2,0:T(8,128)}) fusion(pred[512,2560]{0,1:T(8,128)(4,1)S(1)} %and_and_fusion, bf16[2560,4,128]{2,0,1:T(8,128)(2,1)} %constant_dynamic-update-slice_fusion.7, bf16[512,4,4,128]{3,0,2,1:T(8,128)(2,1)S(1)} %copy-done), kind=kOutput, calls=%fused_computation.183 | convolution fusion | flops 1363151360 | bytes 23470080 | tf_op jit(solution)/shard_map/sub | solution.py:28
  768.9 12.6 %fusion.107 = (f32[4,512]{1,0:T(4,128)S(1)}, f32[4,512,2560]{1,2,0:T(8,128)}) fusion(pred[512,2560]{0,1:T(8,128)(4,1)S(1)} %and_and_fusion, bf16[2560,4,128]{2,0,1:T(8,128)(2,1)} %constant_dynamic-update-slice_fusion.7, bf16[512,4,4,128]{3,0,2,1:T(8,128)(2,1)S(1)} %copy-done), kind=kOutput, calls=%fused_computation.182 | convolution fusion | flops 1363151360 | bytes 23470080 | tf_op jit(solution)/shard_map/sub | solution.py:28
  781.4 12.5 %fusion.106 = (f32[4,512]{1,0:T(4,128)S(1)}, f32[4,512,2560]{1,2,0:T(8,128)}) fusion(pred[512,2560]{0,1:T(8,128)(4,1)S(1)} %and_and_fusion, bf16[2560,4,128]{2,0,1:T(8,128)(2,1)} %constant_dynamic-update-slice_fusion.7, bf16[512,4,4,128]{3,0,2,1:T(8,128)(2,1)S(1)} %copy-done), kind=kOutput, calls=%fused_computation.181 | convolution fusion | flops 1363151360 | bytes 23470080 | tf_op jit(solution)/shard_map/sub | solution.py:28
  794.0 12.7 %fusion.105 = (f32[4,512]{1,0:T(4,128)S(1)}, f32[4,512,2560]{1,2,0:T(8,128)}) fusion(pred[512,2560]{0,1:T(8,128)(4,1)S(1)} %and_and_fusion, bf16[2560,4,128]{2,0,1:T(8,128)(2,1)} %constant_dynamic-update-slice_fusion.7, bf16[512,4,4,128]{3,0,2,1:T(8,128)(2,1)S(1)} %copy-done), kind=kOutput, calls=%fused_computation.180 | convolution fusion | flops 1363151360 | bytes 23470080 | tf_op jit(solution)/shard_map/sub | solution.py:28
  808.6 8.7 %fusion.74 = bf16[128,4,512]{2,0,1:T(8,128)(2,1)S(1)} fusion(f32[4,512,2560]{1,2,0:T(8,128)} %get-tuple-element.33, f32[4,512]{1,0:T(4,128)S(1)} %get-tuple-element.32, bf16[2560,4,128]{2,0,1:T(8,128)(2,1)} %constant_dynamic-update-slice_fusion), kind=kOutput, calls=%fused_computation.94 | convolution fusion | flops 1352925184 | bytes 22159360 | tf_op jit(solution)/shard_map/jqk,kd->qjd/dot_general | solution.py:211
  817.6 8.7 %fusion.73 = bf16[128,4,512]{2,0,1:T(8,128)(2,1)S(1)} fusion(f32[4,512,2560]{1,2,0:T(8,128)} %get-tuple-element.31, f32[4,512]{1,0:T(4,128)S(1)} %get-tuple-element.30, bf16[2560,4,128]{2,0,1:T(8,128)(2,1)} %constant_dynamic-update-slice_fusion), kind=kOutput, calls=%fused_computation.93 | convolution fusion | flops 1352925184 | bytes 22159360 | tf_op jit(solution)/shard_map/jqk,kd->qjd/dot_general | solution.py:211
  826.6 8.7 %fusion.72 = bf16[128,4,512]{2,0,1:T(8,128)(2,1)S(1)} fusion(f32[4,512,2560]{1,2,0:T(8,128)} %get-tuple-element.29, f32[4,512]{1,0:T(4,128)S(1)} %get-tuple-element.28, bf16[2560,4,128]{2,0,1:T(8,128)(2,1)} %constant_dynamic-update-slice_fusion), kind=kOutput, calls=%fused_computation.92 | convolution fusion | flops 1352925184 | bytes 22159360 | tf_op jit(solution)/shard_map/jqk,kd->qjd/dot_general | solution.py:211
  835.5 8.7 %fusion.71 = bf16[128,4,512]{2,0,1:T(8,128)(2,1)S(1)} fusion(f32[4,512,2560]{1,2,0:T(8,128)} %get-tuple-element.27, f32[4,512]{1,0:T(4,128)S(1)} %get-tuple-element.26, bf16[2560,4,128]{2,0,1:T(8,128)(2,1)} %constant_dynamic-update-slice_fusion), kind=kOutput, calls=%fused_computation.91 | convolution fusion | flops 1352925184 | bytes 22159360 | tf_op jit(solution)/shard_map/jqk,kd->qjd/dot_general | solution.py:211
  (128 shorter events, 93.3 us)
Async XLA Ops:
  6.5 212.5 %all-gather.3.cloned.1.call-start = ((), (), s32[]{:S(2)}) async-start(), calls=%async_computation.4 | async-start | bytes 44564480 | tf_op jit(solution)/shard_map/all_gather | solution.py:85
  7.3 289.0 %reduce-scatter.3.cloned.1.call-start = ((), (), s32[]{:S(2)}) async-start(), calls=%async_computation.5 | async-start | bytes 3145728 | tf_op jit(solution)/shard_map/reduce_scatter | solution.py:92
  264.6 31.7 %copy-start.6 = (f32[4096]{0:T(1024)S(1)}, f32[4096]{0:T(1024)}, u32[]{:S(2)}) copy-start(f32[4096]{0:T(1024)} %param.24) | copy-start | bytes 49156
  264.6 316.2 %all-gather.5.cloned.1.call-start = ((), (), s32[]{:S(2)}) async-start(), calls=%async_computation.6 | async-start | bytes 53477376 | tf_op jit(solution)/shard_map/all_gather | solution.py:162
  265.4 40.6 %copy-start.11 = (bf16[1,8,48]{2,1,0:T(8,128)(2,1)S(1)}, bf16[1,8,48]{2,1,0:T(8,128)(2,1)}, u32[]{:S(2)}) copy-start(bf16[1,8,48]{2,1,0:T(8,128)(2,1)} %param.29) | copy-start | bytes 2308
  266.4 33.1 %all-to-all-start = ((s32[16,16,1]{1,2,0:T(1,128)}), s32[16,16,1]{1,2,0:T(1,128)S(1)}, u32[]{:S(2)}, u32[]{:S(2)}) async-start(s32[16,16,1]{1,2,0:T(1,128)} %bitcast), calls=%async_computation | async-start | bytes 16384 | tf_op jit(solution)/shard_map/all_to_all | solution.py:114
  299.5 94.9 %all-to-all-start.1 = ((bf16[16,16,4096]{2,1,0:T(8,128)(2,1)}), bf16[16,16,4096]{2,1,0:T(8,128)(2,1)S(1)}, u32[]{:S(2)}, u32[]{:S(2)}) async-start(bf16[16,16,4096]{2,1,0:T(8,128)(2,1)} %bitcast.12), calls=%async_computation.2 | async-start | bytes 4194304 | tf_op jit(solution)/shard_map/all_to_all | solution.py:113
  305.9 395.9 %reduce-scatter.5.cloned.1.call-start = ((), (), s32[]{:S(2)}) async-start(), calls=%async_computation.7 | async-start | bytes 9437184 | tf_op jit(solution)/shard_map/reduce_scatter | solution.py:173
  394.4 186.4 %copy-start.12 = (f32[4096]{0:T(1024)S(1)}, f32[4096]{0:T(1024)}, u32[]{:S(2)}) copy-start(f32[4096]{0:T(1024)} %param.27) | copy-start | bytes 49156
  614.3 87.5 %copy-start.7 = (f32[4,768]{1,0:T(4,128)S(1)}, f32[4,768]{1,0:T(4,128)}, u32[]{:S(2)}) copy-start(f32[4,768]{1,0:T(4,128)} %param.30) | copy-start | bytes 36868
  614.9 4.8 collective-permute-start.4
  619.8 4.0 collective-permute-start.5
  623.8 14.2 %collective-permute-start.6 = (s32[512]{0:T(512)S(1)}, s32[512]{0:T(512)S(1)}, u32[]{:S(2)}, u32[]{:S(2)}) collective-permute-start(s32[512]{0:T(512)S(1)} %collective-permute-done.5), channel_id=1, source_target_pairs={{0,2},{2,4},{4,6},{6,8},{8,10},{10,12},{12,14},{14,16},{16,18},{18... | collective-permute-start | bytes 6152 | tf_op jit(solution)/shard_map/ppermute | solution.py:22
  638.0 4.9 collective-permute-start.7
  706.2 9.9 %collective-permute-start.8 = (bf16[512,4,128]{2,0,1:T(8,128)(2,1)S(1)}, bf16[512,4,128]{2,0,1:T(8,128)(2,1)S(1)}, u32[]{:S(2)}, u32[]{:S(2)}) collective-permute-start(bf16[512,4,128]{2,0,1:T(8,128)(2,1)S(1)} %get-tuple-element.10), channel_id=1, source_target_pairs={{0,2},{2,4},{4,6},{6,8},{8,10},{10,12},{12,14},{14,16},{16,18},{18... | collective-permute-start | bytes 1572872 | tf_op jit(solution)/shard_map/ppermute | solution.py:22
  710.0 11.7 %collective-permute-start = (bf16[512,4,128]{2,0,1:T(8,128)(2,1)S(1)}, bf16[512,4,128]{2,0,1:T(8,128)(2,1)S(1)}, u32[]{:S(2)}, u32[]{:S(2)}) collective-permute-start(bf16[512,4,128]{2,0,1:T(8,128)(2,1)S(1)} %get-tuple-element.6), channel_id=1, source_target_pairs={{0,2},{2,4},{4,6},{6,8},{8,10},{10,12},{12,14},{14,16},{16,18},{18... | collective-permute-start | bytes 1572872 | tf_op jit(solution)/shard_map/ppermute | solution.py:22
  716.1 11.5 %copy-start.4 = (bf16[512,4,128]{2,0,1:T(8,128)(2,1)}, bf16[512,4,128]{2,0,1:T(8,128)(2,1)S(1)}, u32[]{:S(2)}) copy-start(bf16[512,4,128]{2,0,1:T(8,128)(2,1)S(1)} %collective-permute-done.8) | copy-start | bytes 1572868
  716.1 11.5 %collective-permute-start.9 = (bf16[512,4,128]{2,0,1:T(8,128)(2,1)S(1)}, bf16[512,4,128]{2,0,1:T(8,128)(2,1)}, u32[]{:S(2)}, u32[]{:S(2)}) collective-permute-start(bf16[512,4,128]{2,0,1:T(8,128)(2,1)S(1)} %collective-permute-done.8), channel_id=1, source_target_pairs={{0,2},{2,4},{4,6},{6,8},{8,10},{10,12},{12,14},{14,16},{16,18},{18... | collective-permute-start | bytes 1572872 | tf_op jit(solution)/shard_map/ppermute | solution.py:22
  721.8 11.2 %collective-permute-start.1 = (bf16[512,4,128]{2,0,1:T(8,128)(2,1)S(1)}, bf16[512,4,128]{2,0,1:T(8,128)(2,1)}, u32[]{:S(2)}, u32[]{:S(2)}) collective-permute-start(bf16[512,4,128]{2,0,1:T(8,128)(2,1)S(1)} %collective-permute-done), channel_id=1, source_target_pairs={{0,2},{2,4},{4,6},{6,8},{8,10},{10,12},{12,14},{14,16},{16,18},{18... | collective-permute-start | bytes 1572872 | tf_op jit(solution)/shard_map/ppermute | solution.py:22
  727.7 13.2 %collective-permute-start.10 = (bf16[512,4,128]{2,0,1:T(8,128)(2,1)}, bf16[512,4,128]{2,0,1:T(8,128)(2,1)S(1)}, u32[]{:S(2)}, u32[]{:S(2)}) collective-permute-start(bf16[512,4,128]{2,0,1:T(8,128)(2,1)} %collective-permute-done.9), channel_id=1, source_target_pairs={{0,2},{2,4},{4,6},{6,8},{8,10},{10,12},{12,14},{14,16},{16,18},{18... | collective-permute-start | bytes 1572872 | tf_op jit(solution)/shard_map/ppermute | solution.py:22
  733.0 14.8 %collective-permute-start.2 = (bf16[512,4,128]{2,0,1:T(8,128)(2,1)}, bf16[512,4,128]{2,0,1:T(8,128)(2,1)}, u32[]{:S(2)}, u32[]{:S(2)}) collective-permute-start(bf16[512,4,128]{2,0,1:T(8,128)(2,1)} %collective-permute-done.1), channel_id=1, source_target_pairs={{0,2},{2,4},{4,6},{6,8},{8,10},{10,12},{12,14},{14,16},{16,18},{18... | collective-permute-start | bytes 1572872 | tf_op jit(solution)/shard_map/ppermute | solution.py:22
  740.0 16.3 %copy-start = (bf16[512,4,4,128]{3,0,2,1:T(8,128)(2,1)S(1)}, bf16[512,4,4,128]{3,0,2,1:T(8,128)(2,1)}, u32[]{:S(2)}) copy-start(bf16[512,4,4,128]{3,0,2,1:T(8,128)(2,1)} %fusion.41) | copy-start | bytes 6291460
  740.9 14.5 %collective-permute-start.11 = (bf16[512,4,128]{2,0,1:T(8,128)(2,1)S(1)}, bf16[512,4,128]{2,0,1:T(8,128)(2,1)S(1)}, u32[]{:S(2)}, u32[]{:S(2)}) collective-permute-start(bf16[512,4,128]{2,0,1:T(8,128)(2,1)S(1)} %collective-permute-done.10), channel_id=1, source_target_pairs={{0,2},{2,4},{4,6},{6,8},{8,10},{10,12},{12,14},{14,16},{16,18},{18... | collective-permute-start | bytes 1572872 | tf_op jit(solution)/shard_map/ppermute | solution.py:22
  747.8 58.9 %collective-permute-start.3 = (bf16[512,4,128]{2,0,1:T(8,128)(2,1)}, bf16[512,4,128]{2,0,1:T(8,128)(2,1)}, u32[]{:S(2)}, u32[]{:S(2)}) collective-permute-start(bf16[512,4,128]{2,0,1:T(8,128)(2,1)} %collective-permute-done.2), channel_id=1, source_target_pairs={{0,2},{2,4},{4,6},{6,8},{8,10},{10,12},{12,14},{14,16},{16,18},{18... | collective-permute-start | bytes 1572872 | tf_op jit(solution)/shard_map/ppermute | solution.py:22
  (10 other events, 51.2 us)
Sparse Core Ops, SparseCore 0:
  8.9 210.1 all-gather.2
  264.8 31.4 reduce-scatter.2
  297.8 282.9 all-gather.4
  614.4 87.3 reduce-scatter.4
where the time goes:
time: 861 us; the launch traced here: 853 us
  waiting for transfers between devices  427 us (50%)
  matrix products  160 us (19%)
  blocking collectives  115 us (13%)
  starting transfers between devices  65.9 us (8%)
  other arithmetic  43.4 us (5%)
  local copies, waits for them, and re-layouts  26.5 us (3%)
  between operations  14.6 us (2%)
    all_gather x1, waiting for transfers between devices, on_device(): codes_piece = lax.all_gather(llm_codes, 'ctx', axis=2, tiled=True)  177 us
    all_gather x1, waiting for transfers between devices, merge_project(): codes_piece = lax.all_gather(merger_codes, 'ctx', axis=2, tiled=True)  158 us
    all_gather x1, blocking collectives, on_device(): scale_piece = lax.all_gather(llm_scales, 'ctx', axis=2, tiled=True)  87.5 us
    reduce_scatter x1, waiting for transfers between devices, on_device(): lax.psum_scatter(partial_value.astype(jnp.bfloat16), 'wt', scatter_dimens...  58.9 us
    sub x5, matrix products, softmax_rows(): raised = jnp.exp(masked - highest)  55.8 us
    ppermute x12, starting transfers between devices, passed_along(): lax.ppermute(value, axis, [(source, source + steps) for source in range(l...  54.3 us
    dot_general x4, matrix products, on_device(): jnp.einsum('jqk,kd->qjd', softmaxed, values_all[:, group_index], preferre...  35 us
    dot_general x1, matrix products, on_device(): jnp.dot(normed, dequant_piece.reshape(local_rows, -1), preferred_element_...  33.5 us
  transfers between devices with their start and end apart: 18, of which 10 were waited for; matrix products, arithmetic and copies ran while one was open for 13% of the time, Pallas kernels for 0%

commit v1 on v0

--- a/solution.py
+++ b/solution.py
@@ -82,7 +82,7 @@
 def merge_project(features, merger_codes, merger_scales, merger_bias):
     row_count = features.shape[0]
     flat = features.reshape(row_count, -1)
-    codes_piece = lax.all_gather(merger_codes, "ctx", axis=2, tiled=True)
+    codes_piece = jnp.concatenate(lax.all_gather(merger_codes, "ctx"), axis=2)
     scale_piece = lax.all_gather(merger_scales, "ctx", axis=2, tiled=True)
     width = codes_piece.shape[2]
     dequant = (codes_piece.astype(jnp.float32) * scale_piece.astype(jnp.float32)).astype(

time: 861 us -> 988 us (1.15)
  other arithmetic: 43.4 us -> 132 us
  local copies, waits for them, and re-layouts: 26.5 us -> 64.4 us
    convert_element_type x1, other arithmetic: 28.4 us -> 76.4 us  [merge_project(): (codes_piece.astype(jnp.float32) * scale_piece.astype(jnp.float32)).astyp...]
    convert_element_type x0 -> x1, other arithmetic: none -> 40.6 us  [merge_project(): codes_piece.astype(jnp.float32) * scale_piece.astype(jnp.float32)]
    unnamed x44 -> x45, local copies, waits for them, and re-layouts: 17.7 us -> 55.6 us
  transfers between devices with their start and end apart: 18 -> 18, of which waited for: 10 -> 10; matrix products, arithmetic and copies ran while one was open for 13% -> 11% of each run, Pallas kernels for 0% -> 0%
where the time goes in v1:
time: 988 us; the launch traced here: 979 us
  waiting for transfers between devices  427 us (43%)
  matrix products  160 us (16%)
  other arithmetic  132 us (13%)
  blocking collectives  115 us (12%)
  starting transfers between devices  65.8 us (7%)
  local copies, waits for them, and re-layouts  64.4 us (7%)
  between operations  14.6 us (1%)
    all_gather x1, waiting for transfers between devices, on_device(): codes_piece = lax.all_gather(llm_codes, 'ctx', axis=2, tiled=True)  177 us
    all_gather x1, waiting for transfers between devices, merge_project(): codes_piece = jnp.concatenate(lax.all_gather(merger_codes, 'ctx'), axis=2)  158 us
    all_gather x1, blocking collectives, on_device(): scale_piece = lax.all_gather(llm_scales, 'ctx', axis=2, tiled=True)  87.5 us
    convert_element_type x1, other arithmetic, merge_project(): (codes_piece.astype(jnp.float32) * scale_piece.astype(jnp.float32)).astyp...  76.4 us
    reduce_scatter x1, waiting for transfers between devices, on_device(): lax.psum_scatter(partial_value.astype(jnp.bfloat16), 'wt', scatter_dimens...  59 us
    sub x5, matrix products, softmax_rows(): raised = jnp.exp(masked - highest)  55.8 us
    unnamed x45, local copies, waits for them, and re-layouts  55.6 us
    ppermute x12, starting transfers between devices, passed_along(): lax.ppermute(value, axis, [(source, source + steps) for source in range(l...  54.3 us
  transfers between devices with their start and end apart: 18, of which 10 were waited for; matrix products, arithmetic and copies ran while one was open for 11% of the time, Pallas kernels for 0%

profile of v1, /device:TPU:1, one launch (start us, length us, event | category | flops | bytes accessed | tf_op | source)
XLA Modules:
  0.0 979.5 jit_solution(10207000894229639316)
XLA Ops:
  7.3 8.3 copy.84
  16.6 6.4 add_convert_fusion
  24.2 5.5 fusion.105
  36.8 23.8 %all_gather.17 = bf16[1,1,8192]{2,1,0:T(2,128)(2,1)S(1)} all-gather(bf16[1,1,512]{2,1,0:T(2,128)(2,1)S(1)} %copy-done.10), channel_id=1, replica_groups=mesh['ctx'=16,'wt'=2] {'ctx'}, dimensions={2}, use_global_device_ids=true | all-gather | bytes 17408 | tf_op jit(solution)/shard_map/all_gather | solution.py:86
  60.7 158.4 %all-gather.6.cloned.1.call-done = bf16[64,640,512]{2,1,0:T(8,128)(2,1)} async-done(((bf16[4,640,512]{2,1,0:T(8,128)(2,1)}), bf16[64,640,512]{2,1,0:T(8,128)(2,1)}) %all-gather.6.cloned.1.call-update) | async-done | bytes 41943056 | tf_op jit(solution)/shard_map/all_gather | solution.py:85
  219.1 40.6 %convert.8 = f32[16,4,640,512]{3,2,1,0:T(8,128)} convert(bf16[16,4,640,512]{3,2,1,0:T(8,128)(2,1)} %bitcast.230) | non-fusion elementwise | flops 20971520 | bytes 125829120 | tf_op jit(solution)/shard_map/convert_element_type | solution.py:88
  259.8 76.4 %fusion.5 = bf16[16,4,640,512]{3,0,2,1:T(8,128)(2,1)} fusion(f32[16,4,640,512]{3,2,1,0:T(8,128)} %convert.8, f32[16,512]{1,0:T(8,128)S(1)} %reshape.345), kind=kLoop, calls=%fused_computation.7 | loop fusion | flops 41943040 | bytes 125861888 | tf_op jit(solution)/shard_map/convert_element_type | solution.py:88
  336.2 38.0 %copy.122 = bf16[320,8,16,512]{3,1,2,0:T(8,128)(2,1)} copy(bf16[320,8,16,512]{3,2,1,0:T(8,128)(2,1)} %bitcast.229) | data formatting | bytes 83886080
  374.2 17.2 %convolution_convert_fusion = bf16[128,8192]{1,0:T(8,128)(2,1)} fusion(bf16[128,2560]{1,0:T(8,128)(2,1)S(1)} %reshape_reshape_reshape.3, bf16[2560,8192]{1,0:T(8,128)(2,1)} %bitcast.228), kind=kOutput, calls=%fused_computation.46 | convolution fusion | flops 5369757696 | bytes 44695552 | tf_op jit(solution)/shard_map/dot_general | solution.py:91
  398.2 24.8 %reduce-scatter.3.cloned.1.call-done = bf16[128,4096]{1,0:T(8,128)(2,1)} async-done(((bf16[128,8192]{1,0:T(8,128)(2,1)}), bf16[128,4096]{1,0:T(8,128)(2,1)}) %reduce-scatter.3.cloned.1.call-update) | async-done | bytes 1048592 | tf_op jit(solution)/shard_map/reduce_scatter | solution.py:92
  426.3 6.4 all-to-all-start.1
  432.8 87.5 %all_gather.19 = bf16[1,8,768]{1,0,2:T(2,128)(2,1)S(1)} all-gather(bf16[1,8,48]{1,0,2:T(2,128)(2,1)S(1)} %copy.91), channel_id=1, replica_groups=mesh['ctx'=16,'wt'=2] {'ctx'}, dimensions={2}, use_global_device_ids=true | all-gather | bytes 13056 | tf_op jit(solution)/shard_map/all_gather | solution.py:163
  530.2 177.3 %all-gather.4.cloned.1.call-done = bf16[4096,8,768]{0,2,1:T(8,128)(2,1)} async-done(((bf16[4096,8,48]{0,2,1:T(8,128)(2,1)}), bf16[4096,8,768]{0,2,1:T(8,128)(2,1)}) %all-gather.4.cloned.1.call-update) | async-done | bytes 50331664 | tf_op jit(solution)/shard_map/all_gather | solution.py:162
  707.6 33.5 %fusion.49 = bf16[512,8,768]{2,0,1:T(8,128)(2,1)} fusion(bf16[4096,8,768]{0,2,1:T(8,128)(2,1)} %all-gather.4.cloned.1.call-done, f32[8,768]{1,0:T(8,128)S(1)} %copy.92, bf16[512,4096]{1,0:T(8,128)(2,1)} %get-tuple-element.25, f32[4096]{0:T(1024)S(1)} %copy-done.12, f32[512]{0:T(512)S(1)} %add_rsqrt_fusion), kind=kOutput, calls=%fused_computation.76 | convolution fusion | flops 25856835584 | bytes 60860416 | tf_op jit(solution)/shard_map/dot_general | solution.py:168
  750.6 13.3 %collective-permute-start.6 = (s32[512]{0:T(512)S(1)}, s32[512]{0:T(512)S(1)}, u32[]{:S(2)}, u32[]{:S(2)}) collective-permute-start(s32[512]{0:T(512)S(1)} %collective-permute-done.5), channel_id=1, source_target_pairs={{0,2},{2,4},{4,6},{6,8},{8,10},{10,12},{12,14},{14,16},{16,18},{18... | collective-permute-start | bytes 6152 | tf_op jit(solution)/shard_map/ppermute | solution.py:22
  769.6 59.0 %reduce-scatter.5.cloned.1.call-done = bf16[512,4,768]{2,0,1:T(8,128)(2,1)} async-done(((bf16[512,8,768]{2,0,1:T(8,128)(2,1)}), bf16[512,4,768]{2,0,1:T(8,128)(2,1)}) %reduce-scatter.5.cloned.1.call-update) | async-done | bytes 3145744 | tf_op jit(solution)/shard_map/reduce_scatter | solution.py:173
  883.0 12.6 %fusion.109 = (f32[4,512]{1,0:T(4,128)S(1)}, f32[4,512,2560]{1,2,0:T(8,128)}) fusion(pred[512,2560]{0,1:T(8,128)(4,1)S(1)} %and_and_fusion, bf16[2560,4,128]{2,0,1:T(8,128)(2,1)} %constant_dynamic-update-slice_fusion.7, bf16[512,4,4,128]{3,0,2,1:T(8,128)(2,1)S(1)} %copy-done), kind=kOutput, calls=%fused_computation.185 | convolution fusion | flops 1363151360 | bytes 23470080 | tf_op jit(solution)/shard_map/sub | solution.py:28
  895.6 12.6 %fusion.108 = (f32[4,512]{1,0:T(4,128)S(1)}, f32[4,512,2560]{1,2,0:T(8,128)}) fusion(pred[512,2560]{0,1:T(8,128)(4,1)S(1)} %and_and_fusion, bf16[2560,4,128]{2,0,1:T(8,128)(2,1)} %constant_dynamic-update-slice_fusion.7, bf16[512,4,4,128]{3,0,2,1:T(8,128)(2,1)S(1)} %copy-done), kind=kOutput, calls=%fused_computation.184 | convolution fusion | flops 1363151360 | bytes 23470080 | tf_op jit(solution)/shard_map/sub | solution.py:28
  908.1 12.5 %fusion.107 = (f32[4,512]{1,0:T(4,128)S(1)}, f32[4,512,2560]{1,2,0:T(8,128)}) fusion(pred[512,2560]{0,1:T(8,128)(4,1)S(1)} %and_and_fusion, bf16[2560,4,128]{2,0,1:T(8,128)(2,1)} %constant_dynamic-update-slice_fusion.7, bf16[512,4,4,128]{3,0,2,1:T(8,128)(2,1)S(1)} %copy-done), kind=kOutput, calls=%fused_computation.183 | convolution fusion | flops 1363151360 | bytes 23470080 | tf_op jit(solution)/shard_map/sub | solution.py:28
  920.7 12.7 %fusion.106 = (f32[4,512]{1,0:T(4,128)S(1)}, f32[4,512,2560]{1,2,0:T(8,128)}) fusion(pred[512,2560]{0,1:T(8,128)(4,1)S(1)} %and_and_fusion, bf16[2560,4,128]{2,0,1:T(8,128)(2,1)} %constant_dynamic-update-slice_fusion.7, bf16[512,4,4,128]{3,0,2,1:T(8,128)(2,1)S(1)} %copy-done), kind=kOutput, calls=%fused_computation.182 | convolution fusion | flops 1363151360 | bytes 23470080 | tf_op jit(solution)/shard_map/sub | solution.py:28
  935.3 8.7 fusion.75
  944.2 8.7 fusion.74
  953.2 8.7 fusion.73
  962.2 8.7 fusion.72
  (131 shorter events, 103.3 us)
Async XLA Ops:
  6.5 212.6 %all-gather.6.cloned.1.call-start = ((), (), s32[]{:S(2)}) async-start(), calls=%async_computation.7 | async-start | bytes 44564480 | tf_op jit(solution)/shard_map/all_gather | solution.py:85
  7.3 415.8 %reduce-scatter.3.cloned.1.call-start = ((), (), s32[]{:S(2)}) async-start(), calls=%async_computation.4 | async-start | bytes 3145728 | tf_op jit(solution)/shard_map/reduce_scatter | solution.py:92
  391.4 31.7 %copy-start.6 = (f32[4096]{0:T(1024)S(1)}, f32[4096]{0:T(1024)}, u32[]{:S(2)}) copy-start(f32[4096]{0:T(1024)} %param.24) | copy-start | bytes 49156
  391.4 316.2 %all-gather.4.cloned.1.call-start = ((), (), s32[]{:S(2)}) async-start(), calls=%async_computation.5 | async-start | bytes 53477376 | tf_op jit(solution)/shard_map/all_gather | solution.py:162
  392.1 40.6 %copy-start.11 = (bf16[1,8,48]{2,1,0:T(8,128)(2,1)S(1)}, bf16[1,8,48]{2,1,0:T(8,128)(2,1)}, u32[]{:S(2)}) copy-start(bf16[1,8,48]{2,1,0:T(8,128)(2,1)} %param.29) | copy-start | bytes 2308
  393.2 33.1 %all-to-all-start = ((s32[16,16,1]{1,2,0:T(1,128)}), s32[16,16,1]{1,2,0:T(1,128)S(1)}, u32[]{:S(2)}, u32[]{:S(2)}) async-start(s32[16,16,1]{1,2,0:T(1,128)} %bitcast), calls=%async_computation | async-start | bytes 16384 | tf_op jit(solution)/shard_map/all_to_all | solution.py:114
  426.3 94.9 %all-to-all-start.1 = ((bf16[16,16,4096]{2,1,0:T(8,128)(2,1)}), bf16[16,16,4096]{2,1,0:T(8,128)(2,1)S(1)}, u32[]{:S(2)}, u32[]{:S(2)}) async-start(bf16[16,16,4096]{2,1,0:T(8,128)(2,1)} %bitcast.12), calls=%async_computation.2 | async-start | bytes 4194304 | tf_op jit(solution)/shard_map/all_to_all | solution.py:113
  432.7 395.9 %reduce-scatter.5.cloned.1.call-start = ((), (), s32[]{:S(2)}) async-start(), calls=%async_computation.6 | async-start | bytes 9437184 | tf_op jit(solution)/shard_map/reduce_scatter | solution.py:173
  521.2 186.4 %copy-start.12 = (f32[4096]{0:T(1024)S(1)}, f32[4096]{0:T(1024)}, u32[]{:S(2)}) copy-start(f32[4096]{0:T(1024)} %param.27) | copy-start | bytes 49156
  741.1 87.5 %copy-start.7 = (f32[4,768]{1,0:T(4,128)S(1)}, f32[4,768]{1,0:T(4,128)}, u32[]{:S(2)}) copy-start(f32[4,768]{1,0:T(4,128)} %param.30) | copy-start | bytes 36868
  741.7 4.6 collective-permute-start.4
  746.4 4.2 collective-permute-start.5
  750.6 14.0 %collective-permute-start.6 = (s32[512]{0:T(512)S(1)}, s32[512]{0:T(512)S(1)}, u32[]{:S(2)}, u32[]{:S(2)}) collective-permute-start(s32[512]{0:T(512)S(1)} %collective-permute-done.5), channel_id=1, source_target_pairs={{0,2},{2,4},{4,6},{6,8},{8,10},{10,12},{12,14},{14,16},{16,18},{18... | collective-permute-start | bytes 6152 | tf_op jit(solution)/shard_map/ppermute | solution.py:22
  764.6 5.1 collective-permute-start.7
  833.0 9.9 %collective-permute-start.8 = (bf16[512,4,128]{2,0,1:T(8,128)(2,1)S(1)}, bf16[512,4,128]{2,0,1:T(8,128)(2,1)S(1)}, u32[]{:S(2)}, u32[]{:S(2)}) collective-permute-start(bf16[512,4,128]{2,0,1:T(8,128)(2,1)S(1)} %get-tuple-element.10), channel_id=1, source_target_pairs={{0,2},{2,4},{4,6},{6,8},{8,10},{10,12},{12,14},{14,16},{16,18},{18... | collective-permute-start | bytes 1572872 | tf_op jit(solution)/shard_map/ppermute | solution.py:22
  836.8 11.7 %collective-permute-start = (bf16[512,4,128]{2,0,1:T(8,128)(2,1)S(1)}, bf16[512,4,128]{2,0,1:T(8,128)(2,1)S(1)}, u32[]{:S(2)}, u32[]{:S(2)}) collective-permute-start(bf16[512,4,128]{2,0,1:T(8,128)(2,1)S(1)} %get-tuple-element.6), channel_id=1, source_target_pairs={{0,2},{2,4},{4,6},{6,8},{8,10},{10,12},{12,14},{14,16},{16,18},{18... | collective-permute-start | bytes 1572872 | tf_op jit(solution)/shard_map/ppermute | solution.py:22
  842.9 11.5 %copy-start.4 = (bf16[512,4,128]{2,0,1:T(8,128)(2,1)}, bf16[512,4,128]{2,0,1:T(8,128)(2,1)S(1)}, u32[]{:S(2)}) copy-start(bf16[512,4,128]{2,0,1:T(8,128)(2,1)S(1)} %collective-permute-done.8) | copy-start | bytes 1572868
  842.9 11.5 %collective-permute-start.9 = (bf16[512,4,128]{2,0,1:T(8,128)(2,1)S(1)}, bf16[512,4,128]{2,0,1:T(8,128)(2,1)}, u32[]{:S(2)}, u32[]{:S(2)}) collective-permute-start(bf16[512,4,128]{2,0,1:T(8,128)(2,1)S(1)} %collective-permute-done.8), channel_id=1, source_target_pairs={{0,2},{2,4},{4,6},{6,8},{8,10},{10,12},{12,14},{14,16},{16,18},{18... | collective-permute-start | bytes 1572872 | tf_op jit(solution)/shard_map/ppermute | solution.py:22
  848.5 11.2 %collective-permute-start.1 = (bf16[512,4,128]{2,0,1:T(8,128)(2,1)S(1)}, bf16[512,4,128]{2,0,1:T(8,128)(2,1)}, u32[]{:S(2)}, u32[]{:S(2)}) collective-permute-start(bf16[512,4,128]{2,0,1:T(8,128)(2,1)S(1)} %collective-permute-done), channel_id=1, source_target_pairs={{0,2},{2,4},{4,6},{6,8},{8,10},{10,12},{12,14},{14,16},{16,18},{18... | collective-permute-start | bytes 1572872 | tf_op jit(solution)/shard_map/ppermute | solution.py:22
  854.4 13.2 %collective-permute-start.10 = (bf16[512,4,128]{2,0,1:T(8,128)(2,1)}, bf16[512,4,128]{2,0,1:T(8,128)(2,1)S(1)}, u32[]{:S(2)}, u32[]{:S(2)}) collective-permute-start(bf16[512,4,128]{2,0,1:T(8,128)(2,1)} %collective-permute-done.9), channel_id=1, source_target_pairs={{0,2},{2,4},{4,6},{6,8},{8,10},{10,12},{12,14},{14,16},{16,18},{18... | collective-permute-start | bytes 1572872 | tf_op jit(solution)/shard_map/ppermute | solution.py:22
  859.8 14.8 %collective-permute-start.2 = (bf16[512,4,128]{2,0,1:T(8,128)(2,1)}, bf16[512,4,128]{2,0,1:T(8,128)(2,1)}, u32[]{:S(2)}, u32[]{:S(2)}) collective-permute-start(bf16[512,4,128]{2,0,1:T(8,128)(2,1)} %collective-permute-done.1), channel_id=1, source_target_pairs={{0,2},{2,4},{4,6},{6,8},{8,10},{10,12},{12,14},{14,16},{16,18},{18... | collective-permute-start | bytes 1572872 | tf_op jit(solution)/shard_map/ppermute | solution.py:22
  866.7 16.3 %copy-start = (bf16[512,4,4,128]{3,0,2,1:T(8,128)(2,1)S(1)}, bf16[512,4,4,128]{3,0,2,1:T(8,128)(2,1)}, u32[]{:S(2)}) copy-start(bf16[512,4,4,128]{3,0,2,1:T(8,128)(2,1)} %fusion.42) | copy-start | bytes 6291460
  867.7 14.5 %collective-permute-start.11 = (bf16[512,4,128]{2,0,1:T(8,128)(2,1)S(1)}, bf16[512,4,128]{2,0,1:T(8,128)(2,1)S(1)}, u32[]{:S(2)}, u32[]{:S(2)}) collective-permute-start(bf16[512,4,128]{2,0,1:T(8,128)(2,1)S(1)} %collective-permute-done.10), channel_id=1, source_target_pairs={{0,2},{2,4},{4,6},{6,8},{8,10},{10,12},{12,14},{14,16},{16,18},{18... | collective-permute-start | bytes 1572872 | tf_op jit(solution)/shard_map/ppermute | solution.py:22
  874.5 58.8 %collective-permute-start.3 = (bf16[512,4,128]{2,0,1:T(8,128)(2,1)}, bf16[512,4,128]{2,0,1:T(8,128)(2,1)}, u32[]{:S(2)}, u32[]{:S(2)}) collective-permute-start(bf16[512,4,128]{2,0,1:T(8,128)(2,1)} %collective-permute-done.2), channel_id=1, source_target_pairs={{0,2},{2,4},{4,6},{6,8},{8,10},{10,12},{12,14},{14,16},{16,18},{18... | collective-permute-start | bytes 1572872 | tf_op jit(solution)/shard_map/ppermute | solution.py:22
  (10 other events, 51.2 us)
Sparse Core Ops, SparseCore 0:
  8.9 210.1 all-gather.5
  391.5 31.4 reduce-scatter.2
  424.6 282.9 all-gather.3
  741.2 87.3 reduce-scatter.4
